TPU v7x, 32 devices: a whole 2x2x4 slice. The times are simulated.
32 devices in a mesh: fsdp: 4 (over y, x), ctx: 4 (over z), tp: 2 (over core).
Axes of the slice: x: 2, y: 2, z: 4, core: 2. Of those that a mesh axis runs over, the one named last changes fastest.
Arguments:
- tokens: bfloat16 [8, 1024, 768], P('fsdp', 'ctx'), may hold values from -6 to 6
- lengths: int32 [8], P('fsdp'), may hold values from 256 to 1024, as said below
- cotangent: bfloat16 [8, 1024, 768], P('fsdp', 'ctx'), may hold values from -6 to 6
- ln1_gain: float32 [768], replicated, may hold values from 0.5 to 1.5
- ln1_bias: float32 [768], replicated, may hold values from -1.8 to 1.8
- qkv_weight: bfloat16 [768, 3, 768], P('fsdp', None, 'tp'), may hold values from -0.21875 to 0.21875
- conv_kernel: float32 [3, 3, 768], P(None, None, 'tp'), may hold values from -3.5 to 3.5
- conv_bias: float32 [3, 768], P(None, 'tp'), may hold values from -1.8 to 1.8
- out_weight: bfloat16 [768, 768], P('tp', 'fsdp'), may hold values from -1.75 to 1.75
- ln2_gain: float32 [768], replicated, may hold values from 0.5 to 1.5
- ln2_bias: float32 [768], replicated, may hold values from -1.8 to 1.8
- up_weight: bfloat16 [768, 3072], P('fsdp', 'tp'), may hold values from -0.21875 to 0.21875
- down_weight: bfloat16 [3072, 768], P('tp', 'fsdp'), may hold values from -0.109375 to 0.109375
Outputs:
- result: bfloat16 [8, 1024, 768], P('fsdp', 'ctx')
- input_grad: float32 [8, 1024, 768], P('fsdp', 'ctx')
- ln1_gain_grad: float32 [768], replicated
- ln1_bias_grad: float32 [768], replicated
- qkv_weight_grad: float32 [768, 3, 768], P('fsdp', None, 'tp')
- conv_kernel_grad: float32 [3, 3, 768], P(None, None, 'tp')
- conv_bias_grad: float32 [3, 768], P(None, 'tp')
- out_weight_grad: float32 [768, 768], P('tp', 'fsdp')
- ln2_gain_grad: float32 [768], replicated
- ln2_bias_grad: float32 [768], replicated
- up_weight_grad: float32 [768, 3072], P('fsdp', 'tp')
- down_weight_grad: float32 [3072, 768], P('tp', 'fsdp')
Inputs may be any that keep to these rules, and one draw needn't show every extreme that they name: `lengths`: some slot holds 1024 tokens and some other slot 256.
All inputs are finite; a program needn't handle non-finite values.
Results may differ from a plain program's by a relative error of at most 0.014.
The roundings to bfloat16 on the way count: a program that leaves them out, or rounds other values in their place, can miss the bound.
Values may be sent and summed in bfloat16 or wider, within the bound.
A program may use at most 256 MiB of HBM per device.

v0:
```python
import jax
import jax.numpy as jnp
from jax import lax
from jax.sharding import PartitionSpec as P

HD = 64
EPSILON = 1e-05
SCALING = 0.125
MASKED = -1e30


def shifted(block, axis, distance):
    devices = range(lax.axis_size(axis))
    route = [(i - distance, i) for i in devices if i - distance in devices]
    return lax.ppermute(block, axis, route)


def layer_norm(row_data, norm_gain, shift_bias):
    centred = row_data - jnp.mean(row_data, axis=-1, keepdims=True)
    recip = lax.rsqrt(jnp.mean(centred * centred, axis=-1, keepdims=True) + EPSILON)
    normed = centred * recip
    return (normed * norm_gain + shift_bias, normed, recip)


def norm_back(grad_in, normed, recip, norm_gain):
    scaled = grad_in * norm_gain
    return recip * (
        scaled
        - jnp.mean(scaled, axis=-1, keepdims=True)
        - normed * jnp.mean(scaled * normed, axis=-1, keepdims=True)
    )


def tile_scores(query_part, key_part, query_pos, key_pos, lengths):
    scores = (
        jnp.einsum("mqhd,mkhd->mhqk", query_part, key_part, preferred_element_type=jnp.float32)
        * SCALING
    )
    allowed = (key_pos[None, None, :] <= query_pos[None, :, None]) & (
        key_pos[None, None, :] < lengths[:, None, None]
    )
    return jnp.where(allowed[:, None], scores, MASKED)


def tile_grads(
    query_part, key_part, value_part, grad_part, log_part, delta_part, query_pos, key_pos, lengths
):
    probs_full = jnp.exp(tile_scores(query_part, key_part, query_pos, key_pos, lengths) - log_part)
    prob_grad = jnp.einsum(
        "mqhd,mkhd->mhqk", grad_part, value_part, preferred_element_type=jnp.float32
    )
    score_grad = (probs_full * (prob_grad - delta_part)).astype(jnp.bfloat16)
    return (probs_full, prob_grad, score_grad)


def local(
    tokens,
    lengths,
    cotangent,
    ln1_gain,
    ln1_bias,
    qkv_weight,
    conv_kernel,
    conv_bias,
    out_weight,
    ln2_gain,
    ln2_bias,
    up_weight,
    down_weight,
):
    batches, block_rows, model_width = tokens.shape
    all_rows = batches * block_rows
    qkv_full, out_full, up_full_w, down_full_w = (
        lax.all_gather(qkv_weight, "fsdp", axis=0, tiled=True),
        lax.all_gather(out_weight, "fsdp", axis=1, tiled=True),
        lax.all_gather(up_weight, "fsdp", axis=0, tiled=True),
        lax.all_gather(down_weight, "fsdp", axis=1, tiled=True),
    )
    local_width = qkv_full.shape[2]
    local_heads = local_width // HD
    ctx_count = lax.axis_size("ctx")
    slot_span = block_rows * ctx_count
    group_blocks = 4
    key_span = block_rows * group_blocks
    ctx_index = lax.axis_index("ctx")
    positions = ctx_index * block_rows + jnp.arange(block_rows, dtype=jnp.int32)
    span_iota = jnp.arange(key_span, dtype=jnp.int32)
    block_count = (ctx_index * block_rows + block_rows + key_span - 1) // key_span
    token_valid = positions[None, :] < lengths[:, None]

    def span_slice(array_data, block, axis_pos):
        return lax.dynamic_slice_in_dim(array_data, block * key_span, key_span, axis_pos)

    inputs = tokens.astype(jnp.float32).reshape(all_rows, model_width)
    first_out, first_hat, first_recip = layer_norm(inputs, ln1_gain, ln1_bias)
    first_low = first_out.astype(jnp.bfloat16)
    pre_low = jnp.einsum(
        "td,dcn->tcn", first_low, qkv_full, preferred_element_type=jnp.float32
    ).astype(jnp.bfloat16)
    pre_low = pre_low.reshape(batches, block_rows, 3, local_width)
    earlier = shifted(pre_low[:, block_rows - 2 :], "ctx", 1)
    extended = jnp.concatenate([earlier, pre_low], axis=1).astype(jnp.float32)
    conv_out = (
        conv_bias
        + conv_kernel[0] * extended[:, 2:]
        + conv_kernel[1] * extended[:, 1:-1]
        + conv_kernel[2] * extended[:, :-2]
    ).astype(jnp.bfloat16)
    query_heads = conv_out[:, :, 0].reshape(batches, block_rows, local_heads, HD)
    own_pairs = conv_out[:, :, 1:]
    whole_pairs = lax.all_gather(own_pairs, "ctx", axis=1, tiled=True)
    key_heads = whole_pairs[:, :, 0].reshape(batches, slot_span, local_heads, HD)
    value_heads = whole_pairs[:, :, 1].reshape(batches, slot_span, local_heads, HD)

    def stat_step(block, carry):
        row_max, total = carry
        key_pos = block * key_span + span_iota
        scores = tile_scores(
            query_heads, span_slice(key_heads, block, 1), positions, key_pos, lengths
        )
        new_max = jnp.maximum(row_max, jnp.max(scores, axis=-1, keepdims=True))
        total = total * jnp.exp(row_max - new_max) + jnp.sum(
            jnp.exp(scores - new_max), axis=-1, keepdims=True
        )
        return (new_max, total)

    stat_shape = (batches, local_heads, block_rows, 1)
    row_max, total = lax.fori_loop(
        0,
        block_count,
        stat_step,
        (jnp.full(stat_shape, MASKED, jnp.float32), jnp.zeros(stat_shape, jnp.float32)),
    )
    log_total = row_max + jnp.log(total)

    def value_step(block, accum):
        key_pos = block * key_span + span_iota
        scores = tile_scores(
            query_heads, span_slice(key_heads, block, 1), positions, key_pos, lengths
        )
        probs_low = jnp.exp(scores - log_total).astype(jnp.bfloat16)
        return accum + jnp.einsum(
            "mhqk,mkhd->mqhd",
            probs_low,
            span_slice(value_heads, block, 1),
            preferred_element_type=jnp.float32,
        )

    attn_acc = lax.fori_loop(
        0, block_count, value_step, jnp.zeros((batches, block_rows, local_heads, HD), jnp.float32)
    )
    attn_low = attn_acc.reshape(all_rows, local_width).astype(jnp.bfloat16)
    attn_out = lax.psum(jnp.dot(attn_low, out_full, preferred_element_type=jnp.float32), "tp")
    middle = inputs + attn_out
    second_out, second_hat, second_recip = layer_norm(middle, ln2_gain, ln2_bias)
    second_low = second_out.astype(jnp.bfloat16)
    up_full = jnp.dot(second_low, up_full_w, preferred_element_type=jnp.float32)
    rectified = jnp.maximum(up_full, 0.0)
    act_low = (rectified * rectified).astype(jnp.bfloat16)
    ffn_out = lax.psum(jnp.dot(act_low, down_full_w, preferred_element_type=jnp.float32), "tp")
    result = (middle + ffn_out).reshape(batches, block_rows, model_width).astype(jnp.bfloat16)
    grad_out = (
        cotangent.astype(jnp.float32) * token_valid[:, :, None].astype(jnp.float32)
    ).reshape(all_rows, model_width)
    grad_low = grad_out.astype(jnp.bfloat16)
    down_wgrad = jnp.einsum("tf,td->fd", act_low, grad_low, preferred_element_type=jnp.float32)
    act_grad = jnp.einsum("td,fd->tf", grad_low, down_full_w, preferred_element_type=jnp.float32)
    up_grad_low = (act_grad * 2.0 * rectified).astype(jnp.bfloat16)
    up_wgrad = jnp.einsum("td,tf->df", second_low, up_grad_low, preferred_element_type=jnp.float32)
    second_grad = lax.psum(
        jnp.einsum("tf,df->td", up_grad_low, up_full_w, preferred_element_type=jnp.float32), "tp"
    )
    gain_two_grad = jnp.sum(second_grad * second_hat, axis=0)
    bias_two_grad = jnp.sum(second_grad, axis=0)
    middle_grad = grad_out + norm_back(second_grad, second_hat, second_recip, ln2_gain)
    middle_low = middle_grad.astype(jnp.bfloat16)
    out_wgrad = jnp.einsum("tn,td->nd", attn_low, middle_low, preferred_element_type=jnp.float32)
    attn_flat = jnp.einsum(
        "td,nd->tn", middle_low, out_full, preferred_element_type=jnp.float32
    ).astype(jnp.bfloat16)
    attn_grad = attn_flat.reshape(batches, block_rows, local_heads, HD)

    def delta_step(block, accum):
        key_pos = block * key_span + span_iota
        probs_full = jnp.exp(
            tile_scores(query_heads, span_slice(key_heads, block, 1), positions, key_pos, lengths)
            - log_total
        )
        prob_grad = jnp.einsum(
            "mqhd,mkhd->mhqk",
            attn_grad,
            span_slice(value_heads, block, 1),
            preferred_element_type=jnp.float32,
        )
        return accum + jnp.sum(probs_full * prob_grad, axis=-1, keepdims=True)

    delta = lax.fori_loop(0, block_count, delta_step, jnp.zeros(stat_shape, jnp.float32))
    query_zero = jnp.zeros((batches, block_rows, local_heads, HD), jnp.float32)

    def back_step(block, carry):
        accum, buffer = carry
        key_pos = block * key_span + span_iota
        key_part = span_slice(key_heads, block, 1)
        probs_full, prob_grad, score_grad = tile_grads(
            query_heads,
            key_part,
            span_slice(value_heads, block, 1),
            attn_grad,
            log_total,
            delta,
            positions,
            key_pos,
            lengths,
        )
        probs_again = probs_full.astype(jnp.bfloat16)
        accum = (
            accum
            + jnp.einsum(
                "mhqk,mkhd->mqhd", score_grad, key_part, preferred_element_type=jnp.float32
            )
            * SCALING
        )
        key_term = (
            jnp.einsum(
                "mhqk,mqhd->mkhd", score_grad, query_heads, preferred_element_type=jnp.float32
            )
            * SCALING
        )
        value_term = jnp.einsum(
            "mhqk,mqhd->mkhd", probs_again, attn_grad, preferred_element_type=jnp.float32
        )
        stacked = jnp.stack(
            [
                key_term.reshape(batches, key_span, local_width),
                value_term.reshape(batches, key_span, local_width),
            ],
            axis=2,
        )
        buffer = lax.dynamic_update_slice_in_dim(buffer, stacked, block * key_span, 1)
        return (accum, buffer)

    buffer_zero = jnp.zeros((batches, slot_span, 2, local_width), jnp.float32)
    query_grad, pair_terms = lax.fori_loop(0, block_count, back_step, (query_zero, buffer_zero))
    pair_grad = lax.psum_scatter(pair_terms, "ctx", scatter_dimension=1, tiled=True)
    mixed_grad = jnp.concatenate(
        [query_grad.reshape(batches, block_rows, 1, local_width), pair_grad], axis=2
    )
    later = shifted(mixed_grad[:, :2], "ctx", -1)
    ahead = jnp.concatenate([mixed_grad, later], axis=1)
    pre_grad = (
        conv_kernel[0] * ahead[:, :block_rows]
        + conv_kernel[1] * ahead[:, 1 : block_rows + 1]
        + conv_kernel[2] * ahead[:, 2:]
    ).astype(jnp.bfloat16)
    kernel_grad = jnp.stack(
        [
            jnp.sum(extended[:, 2 - offset : 2 - offset + block_rows] * mixed_grad, axis=(0, 1))
            for offset in range(3)
        ]
    )
    shift_grad = jnp.sum(mixed_grad, axis=(0, 1))
    pre_grad = pre_grad.reshape(all_rows, 3, local_width)
    qkv_wgrad = jnp.einsum("td,tcn->dcn", first_low, pre_grad, preferred_element_type=jnp.float32)
    first_grad = lax.psum(
        jnp.einsum("tcn,dcn->td", pre_grad, qkv_full, preferred_element_type=jnp.float32), "tp"
    )
    gain_one_grad = jnp.sum(first_grad * first_hat, axis=0)
    bias_one_grad = jnp.sum(first_grad, axis=0)
    input_grad = middle_grad + norm_back(first_grad, first_hat, first_recip, ln1_gain)
    input_grad = input_grad.reshape(batches, block_rows, model_width)

    def owned(term, axis_pos):
        part = lax.psum_scatter(
            term.astype(jnp.bfloat16), "fsdp", scatter_dimension=axis_pos, tiled=True
        )
        return lax.psum(part, "ctx").astype(jnp.float32)

    qkv_share = owned(qkv_wgrad, 0)
    out_share = owned(out_wgrad, 1)
    up_share = owned(up_wgrad, 0)
    down_share = owned(down_wgrad, 1)
    small_sums = lax.psum(
        (gain_one_grad, bias_one_grad, kernel_grad, shift_grad, gain_two_grad, bias_two_grad),
        ("fsdp", "ctx"),
    )
    return (
        result,
        input_grad,
        small_sums[0],
        small_sums[1],
        qkv_share,
        small_sums[2],
        small_sums[3],
        out_share,
        small_sums[4],
        small_sums[5],
        up_share,
        down_share,
    )


def solution(mesh):
    placed = (
        P("fsdp", "ctx", None),
        P("fsdp"),
        P("fsdp", "ctx", None),
        P(),
        P(),
        P("fsdp", None, "tp"),
        P(None, None, "tp"),
        P(None, "tp"),
        P("tp", "fsdp"),
        P(),
        P(),
        P("fsdp", "tp"),
        P("tp", "fsdp"),
    )
    return jax.shard_map(
        local,
        mesh=mesh,
        in_specs=placed,
        out_specs=(
            P("fsdp", "ctx", None),
            P("fsdp", "ctx", None),
            P(),
            P(),
            P("fsdp", None, "tp"),
            P(None, None, "tp"),
            P(None, "tp"),
            P("tp", "fsdp"),
            P(),
            P(),
            P("fsdp", "tp"),
            P("tp", "fsdp"),
        ),
        check_vma=False,
    )
```

profile of v0, /device:TPU:0, one launch (start us, length us, event | category | flops | bytes accessed | tf_op | source)
XLA Modules:
  0.0 692.8 jit_solution(6675761201139919809)
XLA Ops:
  8.0 1.3 convert_reduce_fusion
  10.7 34.4 %all-gather.5.cloned.1.call-done = bf16[768,3,384]{2,0,1:T(8,128)(2,1)} async-done(((bf16[192,3,384]{2,0,1:T(8,128)(2,1)}), bf16[768,3,384]{2,0,1:T(8,128)(2,1)}) %all-gather.5.cloned.1.call-update) | async-done | bytes 1769488 | tf_op jit(solution)/shard_map/all_gather | solution.py:74
  45.1 2.7 convolution_convert_fusion.2
  47.8 3.4 collective-permute-start
  53.8 2.1 add_convert_fusion
  56.9 11.0 %all_gather.17 = bf16[384,768]{0,1:T(8,128)(2,1)S(1)} all-gather(bf16[384,192]{0,1:T(8,128)(2,1)S(1)} %copy-done.29), channel_id=1, replica_groups=mesh['fsdp'=4,'ctx'=4,'tp'=2] {'fsdp'}, dimensions={1}, use_global_device_ids=true | all-gather | bytes 737280 | tf_op jit(solution)/shard_map/all_gather | solution.py:75
  68.0 53.2 %all-gather.7.cloned.1.call-done = bf16[2,1024,2,384]{1,3,0,2:T(8,128)(2,1)} async-done(((bf16[2,256,2,384]{1,3,0,2:T(8,128)(2,1)}), bf16[2,1024,2,384]{1,3,0,2:T(8,128)(2,1)}) %all-gather.7.cloned.1.call-update) | async-done | bytes 3145744 | tf_op jit(solution)/shard_map/all_gather | solution.py:111
  121.2 3.5 fusion.71
  124.7 6.7 while.48
  125.3 2.4 fusion.137
  127.7 3.6 exponential_reduce_fusion.2
  132.3 8.3 %while.49 = (s32[]{:T(128)}, f32[2,256,6,64]{1,3,2,0:T(8,128)}, s32[]{:T(128)}, s32[2]{0:T(128)S(1)}, bf16[2,256,6,64]{1,3,2,0:T(8,128)(2,1)S(1)}, /*index=5*/bf...) while((s32[]{:T(128)}, f32[2,256,6,64]{1,3,2,0:T(8,128)}, ...), condition=%wide.region_7.8_spmd.clone, body=%wide.region_6.7_spmd.clone.sunk | while | flops 818875648 | bytes 6715529 | solution.py:149
  133.1 7.6 %fusion.141 = f32[2,256,6,64]{1,3,2,0:T(8,128)} fusion(f32[2,256,6,64]{1,3,2,0:T(8,128)} %get-tuple-element.885, bf16[2,1024,6,64]{1,3,2,0:T(8,128)(2,1)} %get-tuple-element.902, f32[2,6,256]{2,1,0:T(8,128)S(1)} %bitcast.217, pred[2,256,1024]{2,1,0:T(8,128)(4,1)S(1)} %broadcast_and_fusion.9, bf16[2,256,6,64]{1,3,2,0:T(8,128)(2,1)S(1)} %get-tuple-element.899, ...), kind=kOutput, calls=%fused_computation.23.clone.1 | convolution fusion | flops 818085888 | bytes 5648384 | tf_op jit(solution)/shard_map/while/body/mhqk,mkhd->mqhd/dot_general | solution.py:142
  140.6 1.2 convert_element_type.100
  142.3 1.8 fusion.74
  145.7 1.2 copy-done.11
  147.8 15.0 %all-reduce.8.cloned.1.call-done = f32[512,768]{1,0:T(8,128)} async-done(((f32[512,768]{1,0:T(8,128)}), f32[512,768]{1,0:T(8,128)}) %all-reduce.8.cloned.1.call-update) | async-done | bytes 1572880 | tf_op jit(solution)/shard_map/psum | solution.py:153
  162.9 1.8 fusion.70
  165.1 38.1 %all-gather.9.cloned.1.call-done = bf16[768,1536]{1,0:T(8,128)(2,1)} async-done(((bf16[192,1536]{1,0:T(8,128)(2,1)}), bf16[768,1536]{1,0:T(8,128)(2,1)}) %all-gather.9.cloned.1.call-update) | async-done | bytes 2359312 | tf_op jit(solution)/shard_map/all_gather | solution.py:76
  203.1 4.9 convolution_maximum_fusion
  208.0 34.1 %all-gather.11.cloned.1.call-done = bf16[1536,768]{0,1:T(8,128)(2,1)} async-done(((bf16[1536,192]{0,1:T(8,128)(2,1)}), bf16[1536,768]{0,1:T(8,128)(2,1)}) %all-gather.11.cloned.1.call-update) | async-done | bytes 2359312 | tf_op jit(solution)/shard_map/all_gather | solution.py:77
  242.2 4.4 fusion.34
  246.6 1.2 copy-done.64
  247.8 2.6 fusion.75
  250.7 20.2 %all-reduce.10.cloned.1.call-done = f32[512,768]{1,0:T(8,128)} async-done(((f32[512,768]{1,0:T(8,128)}), f32[512,768]{1,0:T(8,128)}) %all-reduce.10.cloned.1.call-update) | async-done | bytes 1572880 | tf_op jit(solution)/shard_map/psum | solution.py:170
  271.0 2.9 multiply_reduce_fusion.4
  276.9 7.2 %while.50 = (s32[]{:T(128)}, f32[2,6,256,1]{2,0,1,3:T(2,128)S(1)}, s32[]{:T(128)}, s32[2]{0:T(128)S(1)}, bf16[2,256,6,64]{1,3,2,0:T(8,128)(2,1)S(1)}, /*index=5*...) while((s32[]{:T(128)}, f32[2,6,256,1]{2,0,1,3:T(2,128)S(1)}, ...), condition=%wide.region_17.18_spmd.clone, body=%wide.region_15.17_spmd.clone.sunk | while | flops 821824768 | bytes 37042348 | solution.py:197
  277.5 1.8 fusion.146
  279.3 4.7 multiply_reduce_fusion.10
  284.9 3.4 broadcast_in_dim.65
  288.4 19.2 %while.51 = (s32[]{:T(128)}, f32[2,256,6,64]{1,3,2,0:T(8,128)S(1)}, f32[2,1024,2,384]{1,3,0,2:T(8,128)}, s32[]{:T(128)}, s32[2]{0:T(128)S(1)}, /*index=5*/bf16[2...) while((s32[]{:T(128)}, f32[2,256,6,64]{1,3,2,0:T(8,128)S(1)}, ...), condition=%wide.region_19.20_spmd.clone, body=%wide.region_18.19_spmd.clone.sunk | while | flops 2048265472 | bytes 87087288 | solution.py:243
  289.3 1.8 fusion.157
  291.2 3.4 fusion.159
  294.6 6.5 multiply_convert_fusion.5
  301.1 2.1 fusion.158
  303.2 1.2 convolution_multiply_fusion.4
  304.4 3.2 pad_maximum_fusion.5
  307.7 1.3 copy-done.8
  309.1 1.4 convolution_convert_fusion.3
  310.6 4.9 convolution_convert_fusion
  315.7 1.5 copy-done.4
  317.2 4.4 convolution_convert_fusion.1
  321.7 98.0 %reduce-scatter.6.cloned.1.call-done = f32[2,256,2,384]{1,3,0,2:T(8,128)} async-done(((f32[2,1024,2,384]{1,3,0,2:T(8,128)}), f32[2,256,2,384]{1,3,0,2:T(8,128)}) %reduce-scatter.6.cloned.1.call-update) | async-done | bytes 1572880 | tf_op jit(solution)/shard_map/reduce_scatter | solution.py:244
  419.7 2.2 fusion.56
  422.0 1.6 copy.74
  423.6 1.3 collective-permute-start.1
  424.9 4.4 collective-permute-done.1
  429.2 1.4 copy.75
  430.7 2.2 pad_maximum_fusion.1
  434.0 4.5 multiply_reduce_fusion.3
  439.5 2.7 bitcast_convert_fusion
  442.3 5.4 fusion.65
  447.7 1.4 copy.76
  449.1 4.2 convolution_bitcast_fusion
  453.5 36.1 %reduce-scatter.14.cloned.1.call-done = bf16[1536,192]{0,1:T(8,128)(2,1)} async-done(((bf16[1536,768]{0,1:T(8,128)(2,1)}), bf16[1536,192]{0,1:T(8,128)(2,1)}) %reduce-scatter.14.cloned.1.call-update) | async-done | bytes 589840 | tf_op jit(solution)/shard_map/reduce_scatter | solution.py:273
  489.6 40.3 %reduce-scatter.12.cloned.1.call-done = bf16[192,1536]{1,0:T(8,128)(2,1)} async-done(((bf16[768,1536]{1,0:T(8,128)(2,1)}), bf16[192,1536]{1,0:T(8,128)(2,1)}) %reduce-scatter.12.cloned.1.call-update) | async-done | bytes 589840 | tf_op jit(solution)/shard_map/reduce_scatter | solution.py:273
  529.9 35.6 %reduce-scatter.8.cloned.1.call-done = bf16[192,3,384]{2,0,1:T(8,128)(2,1)} async-done(((bf16[768,3,384]{2,0,1:T(8,128)(2,1)}), bf16[192,3,384]{2,0,1:T(8,128)(2,1)}) %reduce-scatter.8.cloned.1.call-update) | async-done | bytes 442384 | tf_op jit(solution)/shard_map/reduce_scatter | solution.py:273
  565.5 26.1 %all-reduce.12.cloned.1.call-done = (f32[512,768]{1,0:T(8,128)}, f32[512,768]{1,0:T(8,128)}) async-done(((f32[512,768]{1,0:T(8,128)}, f32[512,768]{1,0:T(8,128)}), (f32[512,768]{1,0:T(8,128)}, f32[512,768]{1,0:T(8,128)})) %all-reduce.12.cloned.1.call-update) | async-done | bytes 3145744 | tf_op jit(solution)/shard_map/psum | solution.py:160
  591.6 2.2 fusion.55
  593.8 81.9 %all-reduce = (f32[768]{0:T(1024)}, f32[768]{0:T(1024)}, f32[3,3,384]{2,1,0:T(4,128)}, f32[3,384]{1,0:T(4,128)}, f32[768]{0:T(1024)}, /*index=5*/f32[768]{0:T(1024)}) all-reduce(f32[768]{0:T(1024)S(1)} %get-tuple-element.486, f32[768]{0:T(1024)S(1)} %get-tuple-element.492, ...), channel_id=1, replica_groups=mesh['fsdp'=4,'ctx'=4,'tp'=2] {'fsdp','ctx'}, use_global_device_ids=true, to_apply=%region_25.26 | all-reduce | flops 7680 | bytes 61440 | tf_op jit(solution)/shard_map/psum | solution.py:282
  675.7 2.6 add_convert_fusion.1
  678.3 1.7 fusion.54
  680.1 1.7 convert_element_type.117
  681.8 2.0 convert_element_type.115
  (221 shorter events, 21.3 us)
Async XLA Ops:
  7.2 2.2 copy-start.5
  7.2 3.1 copy-start.36
  7.2 3.1 copy-start.59
  7.2 37.9 %all-gather.5.cloned.1.call-start = ((), (), s32[]{:S(2)}) async-start(), calls=%async_computation.5 | async-start | bytes 2211840 | tf_op jit(solution)/shard_map/all_gather | solution.py:74
  7.9 113.2 %all-gather.7.cloned.1.call-start = ((), (), s32[]{:S(2)}) async-start(), calls=%async_computation.6 | async-start | bytes 3932160 | tf_op jit(solution)/shard_map/all_gather | solution.py:111
  9.3 38.4 %copy-start.38 = (f32[1,2,2,128]{3,1,2,0:T(2,128)}, f32[1,2,2,128]{3,1,2,0:T(2,128)S(1)}, u32[]{:S(2)}) copy-start(f32[1,2,2,128]{3,1,2,0:T(2,128)S(1)} %copy.100) | copy-start | bytes 6148
  10.3 37.4 %copy-start.40 = (f32[1,2,2,128]{3,1,2,0:T(2,128)}, f32[1,2,2,128]{3,1,2,0:T(2,128)S(1)}, u32[]{:S(2)}) copy-start(f32[1,2,2,128]{3,1,2,0:T(2,128)S(1)} %copy.101) | copy-start | bytes 6148
  10.7 40.5 %copy-start.49 = (f32[3,3,384]{2,1,0:T(4,128)S(1)}, f32[3,3,384]{2,1,0:T(4,128)}, u32[]{:S(2)}) copy-start(f32[3,3,384]{2,1,0:T(4,128)} %param.27) | copy-start | bytes 41476
  47.8 4.8 collective-permute-start
  51.2 2.5 copy-start.30
  51.2 2.5 copy-start.32
  51.3 2.5 copy-start.34
  53.7 2.1 copy-start.1
  55.9 12.1 %copy-start = (bf16[2,256,3,384]{1,3,0,2:T(8,128)(2,1)}, bf16[2,256,3,384]{1,3,0,2:T(8,128)(2,1)S(1)}, u32[]{:S(2)}) copy-start(bf16[2,256,3,384]{1,3,0,2:T(8,128)(2,1)S(1)} %add_convert_fusion) | copy-start | bytes 3538948
  56.8 106.0 %all-reduce.8.cloned.1.call-start = ((), (), s32[]{:S(2)}) async-start(), calls=%async_computation.7 | async-start | bytes 3145728 | tf_op jit(solution)/shard_map/psum | solution.py:153
  68.0 74.3 %copy-start.15 = (bf16[384,768]{0,1:T(8,128)(2,1)}, bf16[384,768]{0,1:T(8,128)(2,1)S(1)}, u32[]{:S(2)}) copy-start(bf16[384,768]{0,1:T(8,128)(2,1)S(1)} %all_gather.17) | copy-start | bytes 1769476
  68.0 56.7 %slice-start = ((bf16[2,256,3,384]{1,3,0,2:T(8,128)(2,1)}), bf16[2,256,1,384]{1,3,0,2:T(8,128)(2,1)S(1)}, s32[]{:S(2)}) async-start(bf16[2,256,3,384]{1,3,0,2:T(8,128)(2,1)} %copy-done), calls=%async_computation.18 | async-start | bytes 786432 | tf_op jit(solution)/shard_map/slice | solution.py:109
  68.0 56.7 %copy-start.28 = (s32[2]{0:T(128)S(1)}, s32[2]{0:T(128)}, u32[]{:S(2)}) copy-start(s32[2]{0:T(128)} %param.22) | copy-start | bytes 28
  140.6 3.5 copy-start.52
  142.3 1.9 copy-start.19
  144.2 59.0 %all-gather.9.cloned.1.call-start = ((), (), s32[]{:S(2)}) async-start(), calls=%async_computation.8 | async-start | bytes 2949120 | tf_op jit(solution)/shard_map/all_gather | solution.py:76
  144.8 97.4 %all-gather.11.cloned.1.call-start = ((), (), s32[]{:S(2)}) async-start(), calls=%async_computation.9 | async-start | bytes 2949120 | tf_op jit(solution)/shard_map/all_gather | solution.py:77
  145.3 125.6 %all-reduce.10.cloned.1.call-start = ((), (), s32[]{:S(2)}) async-start(), calls=%async_computation.10 | async-start | bytes 3145728 | tf_op jit(solution)/shard_map/psum | solution.py:170
  164.7 109.1 %copy-start.3 = (f32[512,768]{1,0:T(8,128)}, f32[512,768]{1,0:T(8,128)S(1)}, u32[]{:S(2)}) copy-start(f32[512,768]{1,0:T(8,128)S(1)} %get-tuple-element.584) | copy-start | bytes 4718596
  164.7 38.4 %copy-start.54 = (f32[768]{0:T(1024)S(1)}, f32[768]{0:T(1024)}, u32[]{:S(2)}) copy-start(f32[768]{0:T(1024)} %param.30) | copy-start | bytes 9220
  164.7 109.1 %copy-start.42 = (f32[512]{0:T(512)}, f32[512]{0:T(512)S(1)}, u32[]{:S(2)}) copy-start(f32[512]{0:T(512)S(1)} %broadcast_multiply_fusion.4) | copy-start | bytes 6148
  165.1 108.8 %copy-start.47 = (f32[512]{0:T(512)}, f32[512]{0:T(512)S(1)}, u32[]{:S(2)}) copy-start(f32[512]{0:T(512)S(1)} %add_rsqrt_fusion) | copy-start | bytes 6148
  242.2 5.6 copy-start.62
  250.5 169.3 %reduce-scatter.6.cloned.1.call-start = ((), (), s32[]{:S(2)}) async-start(), calls=%async_computation.11 | async-start | bytes 7864320 | tf_op jit(solution)/shard_map/reduce_scatter | solution.py:244
  271.0 2.9 copy-start.12
  271.0 2.9 copy-start.14
  277.5 1.8 copy-start.21
  289.3 1.8 copy-start.27
  307.6 3.0 copy-start.23
  307.6 145.8 %reduce-scatter.10.cloned.1.call-start = ((), (), s32[]{:S(2)}) async-start(), calls=%async_computation.13 | async-start | bytes 737280 | tf_op jit(solution)/shard_map/reduce_scatter | solution.py:273
  310.5 179.0 %reduce-scatter.14.cloned.1.call-start = ((), (), s32[]{:S(2)}) async-start(), calls=%async_computation.15 | async-start | bytes 2949120 | tf_op jit(solution)/shard_map/reduce_scatter | solution.py:273
  315.5 1.8 copy-start.55
  315.5 214.4 %reduce-scatter.12.cloned.1.call-start = ((), (), s32[]{:S(2)}) async-start(), calls=%async_computation.14 | async-start | bytes 2949120 | tf_op jit(solution)/shard_map/reduce_scatter | solution.py:273
  321.7 243.7 %reduce-scatter.8.cloned.1.call-start = ((), (), s32[]{:S(2)}) async-start(), calls=%async_computation.12 | async-start | bytes 2211840 | tf_op jit(solution)/shard_map/reduce_scatter | solution.py:273
  423.6 5.7 collective-permute-start.1
  430.7 2.8 copy-start.2
  430.7 3.3 copy-start.10
  430.7 3.3 copy-start.31
  430.7 3.3 copy-start.33
  430.7 3.3 copy-start.35
  434.0 5.5 copy-start.6
  434.0 5.5 copy-start.37
  434.0 5.5 copy-start.57
  434.0 5.5 copy-start.60
  434.0 5.5 copy-start.61
  442.3 5.4 copy-start.18
  442.3 149.3 %all-reduce.12.cloned.1.call-start = ((), (), s32[]{:S(2)}) async-start(), calls=%async_computation.16 | async-start | bytes 6291456 | tf_op jit(solution)/shard_map/psum | solution.py:160
  453.4 112.1 %copy-start.44 = (f32[3,384]{1,0:T(4,128)S(1)}, f32[3,384]{1,0:T(4,128)}, u32[]{:S(2)}) copy-start(f32[3,384]{1,0:T(4,128)} %get-tuple-element.481) | copy-start | bytes 13828
  453.4 112.1 %copy-start.45 = (f32[3,384]{1,0:T(4,128)S(1)}, f32[3,384]{1,0:T(4,128)}, u32[]{:S(2)}) copy-start(f32[3,384]{1,0:T(4,128)} %get-tuple-element.482) | copy-start | bytes 13828
  453.4 112.1 %copy-start.46 = (f32[3,384]{1,0:T(4,128)S(1)}, f32[3,384]{1,0:T(4,128)}, u32[]{:S(2)}) copy-start(f32[3,384]{1,0:T(4,128)} %get-tuple-element.483) | copy-start | bytes 13828
  453.4 138.2 %copy-start.39 = (f32[1,2,2,128]{3,1,2,0:T(2,128)S(1)}, f32[1,2,2,128]{3,1,2,0:T(2,128)}, u32[]{:S(2)}) copy-start(f32[1,2,2,128]{3,1,2,0:T(2,128)} %copy-done.38) | copy-start | bytes 6148
  453.4 138.2 %copy-start.41 = (f32[1,2,2,128]{3,1,2,0:T(2,128)S(1)}, f32[1,2,2,128]{3,1,2,0:T(2,128)}, u32[]{:S(2)}) copy-start(f32[1,2,2,128]{3,1,2,0:T(2,128)} %copy-done.40) | copy-start | bytes 6148
  453.4 226.6 %all-reduce.14.cloned.1.call-start = ((), (), s32[]{:S(2)}) async-start(), calls=%async_computation.17 | async-start | bytes 3538944 | tf_op jit(solution)/shard_map/psum | solution.py:276
  565.5 28.4 %copy-start.50 = (f32[768]{0:T(1024)S(1)}, f32[768]{0:T(1024)}, u32[]{:S(2)}) copy-start(f32[768]{0:T(1024)} %get-tuple-element.484) | copy-start | bytes 9220
  565.5 28.4 %copy-start.51 = (f32[768]{0:T(1024)S(1)}, f32[768]{0:T(1024)}, u32[]{:S(2)}) copy-start(f32[768]{0:T(1024)} %get-tuple-element.491) | copy-start | bytes 9220
  675.7 2.6 copy-start.9
  675.7 2.6 copy-start.13
  680.0 3.8 copy-start.25
  681.8 3.2 copy-start.24
  (17 other events, 22.0 us)
Sparse Core Ops, SparseCore 0:
  9.9 35.1 all-gather.4
  57.0 64.1 all-gather.6
  144.3 18.5 all-reduce.7
  164.6 38.5 all-gather.8
  204.8 37.3 all-gather.10
  250.6 20.3 all-reduce.9
  307.8 111.9 reduce-scatter.5
  423.2 25.8 reduce-scatter.9
  452.2 37.3 reduce-scatter.13
  492.5 37.3 reduce-scatter.11
  532.9 32.4 reduce-scatter.7
  568.2 23.3 all-reduce.11
  594.3 78.6 all-reduce.13
where the time goes:
time: 700 us; the launch traced here: 693 us
  waiting for transfers between devices  438 us (63%)
  blocking collectives  92.9 us (13%)
  matrix products  71.5 us (10%)
  other arithmetic  43.9 us (6%)
  local copies, waits for them, and re-layouts  25.2 us (4%)
  between operations  15 us (2%)
    reduce_scatter x4, waiting for transfers between devices, owned(): lax.psum_scatter(term.astype(jnp.bfloat16), 'fsdp', scatter_dimension=axi...  112 us
    reduce_scatter x1, waiting for transfers between devices, local(): lax.psum_scatter(pair_terms, 'ctx', scatter_dimension=1, tiled=True)  98 us
    psum x1, blocking collectives, local(): lax.psum((gain_one_grad, bias_one_grad, kernel_grad, shift_grad, gain_two...  81.9 us
    all_gather x1, waiting for transfers between devices, local(): whole_pairs = lax.all_gather(own_pairs, 'ctx', axis=1, tiled=True)  53.2 us
    all_gather x1, waiting for transfers between devices, local(): lax.all_gather(up_weight, 'fsdp', axis=0, tiled=True)  38.1 us
    all_gather x1, waiting for transfers between devices, local(): lax.all_gather(qkv_weight, 'fsdp', axis=0, tiled=True)  34.4 us
    all_gather x1, waiting for transfers between devices, local(): lax.all_gather(down_weight, 'fsdp', axis=1, tiled=True)  34.1 us
    psum x1, waiting for transfers between devices, local(): lax.psum(jnp.dot(act_low, down_full_w, preferred_element_type=jnp.float32...  26.1 us
  transfers between devices with their start and end apart: 15, of which 13 were waited for; matrix products, arithmetic and copies ran while one was open for 8% of the time, Pallas kernels for 0%

commit v1 on v0

--- a/solution.py
+++ b/solution.py
@@ -7,6 +7,19 @@
 EPSILON = 1e-05
 SCALING = 0.125
 MASKED = -1e30
+
+
+def collect(x, axis, dim):
+    ways = lax.axis_size(axis)
+    up = [(d, (d + 1) % ways) for d in range(ways)]
+    down = [(d, (d - 1) % ways) for d in range(ways)]
+    earlier, later = ([x], [x])
+    for _ in range(ways // 2):
+        earlier.append(lax.ppermute(earlier[-1], axis, up))
+    for _ in range((ways - 1) // 2):
+        later.append(lax.ppermute(later[-1], axis, down))
+    line = jnp.concatenate([*earlier[::-1], *later[1:]], axis=dim)
+    return jnp.roll(line, (lax.axis_index(axis) - ways // 2) * x.shape[dim], axis=dim)
 
 
 def shifted(block, axis, distance):
@@ -71,7 +84,7 @@
     batches, block_rows, model_width = tokens.shape
     all_rows = batches * block_rows
     qkv_full, out_full, up_full_w, down_full_w = (
-        lax.all_gather(qkv_weight, "fsdp", axis=0, tiled=True),
+        collect(qkv_weight, "fsdp", 0),
         lax.all_gather(out_weight, "fsdp", axis=1, tiled=True),
         lax.all_gather(up_weight, "fsdp", axis=0, tiled=True),
         lax.all_gather(down_weight, "fsdp", axis=1, tiled=True),

time: 700 us -> 678 us (0.969)
  waiting for transfers between devices: 438 us -> 405 us
    all_gather x1 -> x0, waiting for transfers between devices: 34.4 us -> none  [local(): lax.all_gather(qkv_weight, 'fsdp', axis=0, tiled=True)]
    ppermute x0 -> x3, waiting for transfers between devices: none -> 23.2 us  [the longest x2 23.2 us: collect(): earlier.append(lax.ppermute(earlier[-1], axis, up))]
    all_gather x1, waiting for transfers between devices: 38.1 us -> 16.9 us  [local(): lax.all_gather(up_weight, 'fsdp', axis=0, tiled=True)]
  transfers between devices with their start and end apart: 15 -> 17, of which waited for: 13 -> 14; matrix products, arithmetic and copies ran while one was open for 8% -> 8% of each run, Pallas kernels for 0% -> 0%
where the time goes in v1:
time: 678 us; the launch traced here: 670 us
  waiting for transfers between devices  405 us (60%)
  blocking collectives  93 us (14%)
  matrix products  69.9 us (10%)
  other arithmetic  47.1 us (7%)
  local copies, waits for them, and re-layouts  25.8 us (4%)
  between operations  16.7 us (2%)
  starting transfers between devices  11 us (2%)
    reduce_scatter x4, waiting for transfers between devices, owned(): lax.psum_scatter(term.astype(jnp.bfloat16), 'fsdp', scatter_dimension=axi...  112 us
    reduce_scatter x1, waiting for transfers between devices, local(): lax.psum_scatter(pair_terms, 'ctx', scatter_dimension=1, tiled=True)  98 us
    psum x1, blocking collectives, local(): lax.psum((gain_one_grad, bias_one_grad, kernel_grad, shift_grad, gain_two...  81.9 us
    all_gather x1, waiting for transfers between devices, local(): whole_pairs = lax.all_gather(own_pairs, 'ctx', axis=1, tiled=True)  53.4 us
    all_gather x1, waiting for transfers between devices, local(): lax.all_gather(down_weight, 'fsdp', axis=1, tiled=True)  34.2 us
    psum x1, waiting for transfers between devices, local(): lax.psum(jnp.dot(act_low, down_full_w, preferred_element_type=jnp.float32...  26.3 us
    ppermute x2, waiting for transfers between devices, collect(): earlier.append(lax.ppermute(earlier[-1], axis, up))  23.2 us
    psum x1, waiting for transfers between devices, local(): lax.psum(jnp.einsum('tf,df->td', up_grad_low, up_full_w, preferred_elemen...  20.3 us
  transfers between devices with their start and end apart: 17, of which 14 were waited for; matrix products, arithmetic and copies ran while one was open for 8% of the time, Pallas kernels for 0%

profile of v1, /device:TPU:0, one launch (start us, length us, event | category | flops | bytes accessed | tf_op | source)
XLA Modules:
  0.0 669.6 jit_solution(10560588730723999708)
XLA Ops:
  8.1 3.0 collective-permute-start
  12.1 1.3 convert_reduce_fusion
  13.5 1.5 fusion.40
  15.0 8.3 %collective-permute-done = bf16[192,3,384]{2,0,1:T(8,128)(2,1)S(1)} collective-permute-done((bf16[192,3,384]{2,0,1:T(8,128)(2,1)}, bf16[192,3,384]{2,0,1:T(8,128)(2,1)S(1)}, u32[]{:S(2)}, u32[]{:S(2)}) %collective-permute-start) | collective-permute-done | bytes 442400 | tf_op jit(solution)/shard_map/ppermute | solution.py:18
  24.9 1.5 fusion.50
  26.5 14.9 %collective-permute-done.1 = bf16[192,3,384]{2,0,1:T(8,128)(2,1)S(1)} collective-permute-done((bf16[192,3,384]{2,0,1:T(8,128)(2,1)S(1)}, bf16[192,3,384]{2,0,1:T(8,128)(2,1)S(1)}, u32[]{:S(2)}, u32[]{:S(2)}) %collective-permute-start.1) | collective-permute-done | bytes 442400 | tf_op jit(solution)/shard_map/ppermute | solution.py:18
  43.9 3.7 collective-permute-start.3
  50.1 2.1 add_convert_fusion
  53.2 11.1 %all_gather.13 = bf16[384,768]{0,1:T(8,128)(2,1)S(1)} all-gather(bf16[384,192]{0,1:T(8,128)(2,1)S(1)} %copy-done.27), channel_id=1, replica_groups=mesh['fsdp'=4,'ctx'=4,'tp'=2] {'fsdp'}, dimensions={1}, use_global_device_ids=true | all-gather | bytes 737280 | tf_op jit(solution)/shard_map/all_gather | solution.py:88
  64.4 53.4 %all-gather.4.cloned.1.call-done = bf16[2,1024,2,384]{1,3,0,2:T(8,128)(2,1)} async-done(((bf16[2,256,2,384]{1,3,0,2:T(8,128)(2,1)}), bf16[2,1024,2,384]{1,3,0,2:T(8,128)(2,1)}) %all-gather.4.cloned.1.call-update) | async-done | bytes 3145744 | tf_op jit(solution)/shard_map/all_gather | solution.py:124
  117.8 3.5 fusion.83
  121.3 6.7 while.48
  121.9 2.4 fusion.147
  124.3 3.6 exponential_reduce_fusion.2
  128.9 8.3 %while.49 = (s32[]{:T(128)}, f32[2,256,6,64]{1,3,2,0:T(8,128)}, s32[]{:T(128)}, s32[2]{0:T(128)S(1)}, bf16[2,256,6,64]{1,3,2,0:T(8,128)(2,1)S(1)}, /*index=5*/bf...) while((s32[]{:T(128)}, f32[2,256,6,64]{1,3,2,0:T(8,128)}, ...), condition=%wide.region_7.8_spmd.clone, body=%wide.region_6.7_spmd.clone.sunk | while | flops 818875648 | bytes 6715529 | solution.py:162
  129.7 7.6 %fusion.151 = f32[2,256,6,64]{1,3,2,0:T(8,128)} fusion(f32[2,256,6,64]{1,3,2,0:T(8,128)} %get-tuple-element.885, bf16[2,1024,6,64]{1,3,2,0:T(8,128)(2,1)} %get-tuple-element.902, f32[2,6,256]{2,1,0:T(8,128)S(1)} %bitcast.215, pred[2,256,1024]{2,1,0:T(8,128)(4,1)S(1)} %broadcast_and_fusion.9, bf16[2,256,6,64]{1,3,2,0:T(8,128)(2,1)S(1)} %get-tuple-element.899, ...), kind=kOutput, calls=%fused_computation.23.clone.1 | convolution fusion | flops 818085888 | bytes 5648384 | tf_op jit(solution)/shard_map/while/body/mhqk,mkhd->mqhd/dot_general | solution.py:155
  138.9 1.7 fusion.86
  144.3 15.1 %all-reduce.8.cloned.1.call-done = f32[512,768]{1,0:T(8,128)} async-done(((f32[512,768]{1,0:T(8,128)}), f32[512,768]{1,0:T(8,128)}) %all-reduce.8.cloned.1.call-update) | async-done | bytes 1572880 | tf_op jit(solution)/shard_map/psum | solution.py:166
  159.4 1.8 fusion.82
  161.6 16.9 %all-gather.6.cloned.1.call-done = bf16[768,1536]{1,0:T(8,128)(2,1)} async-done(((bf16[192,1536]{1,0:T(8,128)(2,1)}), bf16[768,1536]{1,0:T(8,128)(2,1)}) %all-gather.6.cloned.1.call-update) | async-done | bytes 2359312 | tf_op jit(solution)/shard_map/all_gather | solution.py:89
  178.5 4.8 convolution_maximum_fusion
  183.2 34.2 %all-gather.8.cloned.1.call-done = bf16[1536,768]{0,1:T(8,128)(2,1)} async-done(((bf16[1536,192]{0,1:T(8,128)(2,1)}), bf16[1536,768]{0,1:T(8,128)(2,1)}) %all-gather.8.cloned.1.call-update) | async-done | bytes 2359312 | tf_op jit(solution)/shard_map/all_gather | solution.py:90
  217.4 4.4 fusion.34
  223.0 2.6 fusion.87
  225.8 20.3 %all-reduce.10.cloned.1.call-done = f32[512,768]{1,0:T(8,128)} async-done(((f32[512,768]{1,0:T(8,128)}), f32[512,768]{1,0:T(8,128)}) %all-reduce.10.cloned.1.call-update) | async-done | bytes 1572880 | tf_op jit(solution)/shard_map/psum | solution.py:183
  246.1 2.9 multiply_reduce_fusion.4
  251.8 7.2 %while.50 = (s32[]{:T(128)}, f32[2,6,256,1]{2,0,1,3:T(2,128)S(1)}, s32[]{:T(128)}, s32[2]{0:T(128)S(1)}, bf16[2,256,6,64]{1,3,2,0:T(8,128)(2,1)S(1)}, /*index=5*...) while((s32[]{:T(128)}, f32[2,6,256,1]{2,0,1,3:T(2,128)S(1)}, ...), condition=%wide.region_17.18_spmd.clone, body=%wide.region_15.17_spmd.clone.sunk | while | flops 821824768 | bytes 37042348 | solution.py:210
  252.4 1.8 fusion.156
  254.2 4.7 multiply_reduce_fusion.10
  259.8 3.4 broadcast_in_dim.65
  263.2 19.2 %while.51 = (s32[]{:T(128)}, f32[2,256,6,64]{1,3,2,0:T(8,128)S(1)}, f32[2,1024,2,384]{1,3,0,2:T(8,128)}, s32[]{:T(128)}, s32[2]{0:T(128)S(1)}, /*index=5*/bf16[2...) while((s32[]{:T(128)}, f32[2,256,6,64]{1,3,2,0:T(8,128)S(1)}, ...), condition=%wide.region_19.20_spmd.clone, body=%wide.region_18.19_spmd.clone.sunk | while | flops 2048265472 | bytes 87087288 | solution.py:256
  264.2 1.8 fusion.167
  266.1 3.4 fusion.169
  269.5 6.5 multiply_convert_fusion.5
  276.0 2.1 fusion.168
  279.3 3.2 pad_maximum_fusion.5
  282.6 1.3 copy-done.6
  283.9 1.4 convolution_convert_fusion.2
  285.5 4.9 convolution_convert_fusion
  290.6 1.5 copy-done.3
  292.1 4.5 convolution_convert_fusion.1
  296.6 98.0 %reduce-scatter.6.cloned.1.call-done = f32[2,256,2,384]{1,3,0,2:T(8,128)} async-done(((f32[2,1024,2,384]{1,3,0,2:T(8,128)}), f32[2,256,2,384]{1,3,0,2:T(8,128)}) %reduce-scatter.6.cloned.1.call-update) | async-done | bytes 1572880 | tf_op jit(solution)/shard_map/reduce_scatter | solution.py:257
  394.6 2.2 fusion.66
  396.8 1.6 copy.74
  398.5 1.3 collective-permute-start.4
  399.8 4.4 collective-permute-done.4
  404.1 1.4 copy.75
  405.6 2.2 pad_maximum_fusion.1
  408.9 4.5 multiply_reduce_fusion.3
  414.4 2.7 bitcast_convert_fusion
  417.2 5.4 fusion.75
  422.6 1.4 copy.76
  424.0 4.2 fusion.63
  428.4 35.8 %reduce-scatter.14.cloned.1.call-done = bf16[1536,192]{0,1:T(8,128)(2,1)} async-done(((bf16[1536,768]{0,1:T(8,128)(2,1)}), bf16[1536,192]{0,1:T(8,128)(2,1)}) %reduce-scatter.14.cloned.1.call-update) | async-done | bytes 589840 | tf_op jit(solution)/shard_map/reduce_scatter | solution.py:286
  464.2 40.4 %reduce-scatter.12.cloned.1.call-done = bf16[192,1536]{1,0:T(8,128)(2,1)} async-done(((bf16[768,1536]{1,0:T(8,128)(2,1)}), bf16[192,1536]{1,0:T(8,128)(2,1)}) %reduce-scatter.12.cloned.1.call-update) | async-done | bytes 589840 | tf_op jit(solution)/shard_map/reduce_scatter | solution.py:286
  504.6 35.5 %reduce-scatter.8.cloned.1.call-done = bf16[192,3,384]{2,0,1:T(8,128)(2,1)} async-done(((bf16[768,3,384]{2,0,1:T(8,128)(2,1)}), bf16[192,3,384]{2,0,1:T(8,128)(2,1)}) %reduce-scatter.8.cloned.1.call-update) | async-done | bytes 442384 | tf_op jit(solution)/shard_map/reduce_scatter | solution.py:286
  540.2 26.3 %all-reduce.12.cloned.1.call-done = (f32[512,768]{1,0:T(8,128)}, f32[512,768]{1,0:T(8,128)}) async-done(((f32[512,768]{1,0:T(8,128)}, f32[512,768]{1,0:T(8,128)}), (f32[512,768]{1,0:T(8,128)}, f32[512,768]{1,0:T(8,128)})) %all-reduce.12.cloned.1.call-update) | async-done | bytes 3145744 | tf_op jit(solution)/shard_map/psum | solution.py:173
  566.5 2.2 fusion.55
  568.7 81.9 %all-reduce = (f32[768]{0:T(1024)}, f32[768]{0:T(1024)}, f32[3,3,384]{2,1,0:T(4,128)}, f32[3,384]{1,0:T(4,128)}, f32[768]{0:T(1024)}, /*index=5*/f32[768]{0:T(1024)}) all-reduce(f32[768]{0:T(1024)S(1)} %get-tuple-element.486, f32[768]{0:T(1024)S(1)} %get-tuple-element.492, ...), channel_id=1, replica_groups=mesh['fsdp'=4,'ctx'=4,'tp'=2] {'fsdp','ctx'}, use_global_device_ids=true, to_apply=%region_25.26 | all-reduce | flops 7680 | bytes 61440 | tf_op jit(solution)/shard_map/psum | solution.py:295
  650.6 2.6 add_convert_fusion.1
  653.2 1.7 fusion.54
  654.9 1.7 convert_element_type.117
  656.6 2.0 convert_element_type.115
  658.6 2.2 convert_element_type.119
  (225 shorter events, 27.5 us)
Async XLA Ops:
  8.0 33.5 %copy-start.19 = (bf16[192,3,384]{2,0,1:T(8,128)(2,1)S(1)}, bf16[192,3,384]{2,0,1:T(8,128)(2,1)}, u32[]{:S(2)}) copy-start(bf16[192,3,384]{2,0,1:T(8,128)(2,1)} %param.26) | copy-start | bytes 1327108
  8.0 109.8 %all-gather.4.cloned.1.call-start = ((), (), s32[]{:S(2)}) async-start(), calls=%async_computation.5 | async-start | bytes 3932160 | tf_op jit(solution)/shard_map/all_gather | solution.py:124
  8.1 15.2 %collective-permute-start = (bf16[192,3,384]{2,0,1:T(8,128)(2,1)}, bf16[192,3,384]{2,0,1:T(8,128)(2,1)S(1)}, u32[]{:S(2)}, u32[]{:S(2)}) collective-permute-start(bf16[192,3,384]{2,0,1:T(8,128)(2,1)} %param.26), channel_id=1, source_target_pairs={{0,8},{8,16},{16,24},{24,0},{1,9},{9,17},{17,25},{25,1},{2,10},{10... | collective-permute-start | bytes 1327112 | tf_op jit(solution)/shard_map/ppermute | solution.py:18
  11.1 30.5 %collective-permute-start.2 = (bf16[192,3,384]{2,0,1:T(8,128)(2,1)}, bf16[192,3,384]{2,0,1:T(8,128)(2,1)S(1)}, u32[]{:S(2)}, u32[]{:S(2)}) collective-permute-start(bf16[192,3,384]{2,0,1:T(8,128)(2,1)} %param.26), channel_id=1, source_target_pairs={{0,24},{8,0},{16,8},{24,16},{1,25},{9,1},{17,9},{25,17},{2,26},{10... | collective-permute-start | bytes 1327112 | tf_op jit(solution)/shard_map/ppermute | solution.py:20
  13.4 28.2 %copy-start.36 = (f32[1,2,2,128]{3,1,2,0:T(2,128)}, f32[1,2,2,128]{3,1,2,0:T(2,128)S(1)}, u32[]{:S(2)}) copy-start(f32[1,2,2,128]{3,1,2,0:T(2,128)S(1)} %copy.100) | copy-start | bytes 6148
  23.3 18.1 %collective-permute-start.1 = (bf16[192,3,384]{2,0,1:T(8,128)(2,1)S(1)}, bf16[192,3,384]{2,0,1:T(8,128)(2,1)S(1)}, u32[]{:S(2)}, u32[]{:S(2)}) collective-permute-start(bf16[192,3,384]{2,0,1:T(8,128)(2,1)S(1)} %collective-permute-done), channel_id=1, source_target_pairs={{0,8},{8,16},{16,24},{24,0},{1,9},{9,17},{17,25},{25,1},{2,10},{10... | collective-permute-start | bytes 1327112 | tf_op jit(solution)/shard_map/ppermute | solution.py:18
  24.9 16.8 %copy-start.38 = (f32[1,2,2,128]{3,1,2,0:T(2,128)}, f32[1,2,2,128]{3,1,2,0:T(2,128)S(1)}, u32[]{:S(2)}) copy-start(f32[1,2,2,128]{3,1,2,0:T(2,128)S(1)} %copy.101) | copy-start | bytes 6148
  42.0 1.8 copy-start.34
  42.0 5.5 copy-start.47
  43.9 5.0 collective-permute-start.3
  47.6 2.5 copy-start.28
  47.6 2.5 copy-start.30
  47.6 2.5 copy-start.32
  50.1 2.1 copy-start
  53.2 106.2 %all-reduce.8.cloned.1.call-start = ((), (), s32[]{:S(2)}) async-start(), calls=%async_computation.6 | async-start | bytes 3145728 | tf_op jit(solution)/shard_map/psum | solution.py:166
  64.3 74.6 %copy-start.13 = (bf16[384,768]{0,1:T(8,128)(2,1)}, bf16[384,768]{0,1:T(8,128)(2,1)S(1)}, u32[]{:S(2)}) copy-start(bf16[384,768]{0,1:T(8,128)(2,1)S(1)} %all_gather.13) | copy-start | bytes 1769476
  64.4 56.9 %copy-start.26 = (s32[2]{0:T(128)S(1)}, s32[2]{0:T(128)}, u32[]{:S(2)}) copy-start(s32[2]{0:T(128)} %param.22) | copy-start | bytes 28
  138.9 2.4 copy-start.17
  140.7 37.8 %all-gather.6.cloned.1.call-start = ((), (), s32[]{:S(2)}) async-start(), calls=%async_computation.7 | async-start | bytes 2949120 | tf_op jit(solution)/shard_map/all_gather | solution.py:89
  141.3 76.1 %all-gather.8.cloned.1.call-start = ((), (), s32[]{:S(2)}) async-start(), calls=%async_computation.8 | async-start | bytes 2949120 | tf_op jit(solution)/shard_map/all_gather | solution.py:90
  141.9 104.2 %all-reduce.10.cloned.1.call-start = ((), (), s32[]{:S(2)}) async-start(), calls=%async_computation.9 | async-start | bytes 3145728 | tf_op jit(solution)/shard_map/psum | solution.py:183
  144.3 34.1 %copy-start.52 = (f32[768]{0:T(1024)S(1)}, f32[768]{0:T(1024)}, u32[]{:S(2)}) copy-start(f32[768]{0:T(1024)} %param.30) | copy-start | bytes 9220
  161.2 87.7 %copy-start.2 = (f32[512,768]{1,0:T(8,128)}, f32[512,768]{1,0:T(8,128)S(1)}, u32[]{:S(2)}) copy-start(f32[512,768]{1,0:T(8,128)S(1)} %get-tuple-element.584) | copy-start | bytes 4718596
  161.3 87.7 %copy-start.40 = (f32[512]{0:T(512)}, f32[512]{0:T(512)S(1)}, u32[]{:S(2)}) copy-start(f32[512]{0:T(512)S(1)} %broadcast_multiply_fusion.4) | copy-start | bytes 6148
  161.6 87.4 %copy-start.45 = (f32[512]{0:T(512)}, f32[512]{0:T(512)S(1)}, u32[]{:S(2)}) copy-start(f32[512]{0:T(512)S(1)} %add_rsqrt_fusion) | copy-start | bytes 6148
  217.4 5.5 copy-start.59
  225.6 169.0 %reduce-scatter.6.cloned.1.call-start = ((), (), s32[]{:S(2)}) async-start(), calls=%async_computation.10 | async-start | bytes 7864320 | tf_op jit(solution)/shard_map/reduce_scatter | solution.py:257
  246.1 2.9 copy-start.10
  246.1 2.9 copy-start.12
  249.0 1.8 copy-start.14
  252.4 1.8 copy-start.20
  264.2 1.8 copy-start.25
  282.5 3.0 copy-start.22
  282.5 145.8 %reduce-scatter.10.cloned.1.call-start = ((), (), s32[]{:S(2)}) async-start(), calls=%async_computation.12 | async-start | bytes 737280 | tf_op jit(solution)/shard_map/reduce_scatter | solution.py:286
  285.4 178.8 %reduce-scatter.14.cloned.1.call-start = ((), (), s32[]{:S(2)}) async-start(), calls=%async_computation.14 | async-start | bytes 2949120 | tf_op jit(solution)/shard_map/reduce_scatter | solution.py:286
  290.3 1.8 copy-start.41
  290.3 1.8 copy-start.46
  290.3 1.8 copy-start.53
  290.4 214.2 %reduce-scatter.12.cloned.1.call-start = ((), (), s32[]{:S(2)}) async-start(), calls=%async_computation.13 | async-start | bytes 2949120 | tf_op jit(solution)/shard_map/reduce_scatter | solution.py:286
  296.6 243.5 %reduce-scatter.8.cloned.1.call-start = ((), (), s32[]{:S(2)}) async-start(), calls=%async_computation.11 | async-start | bytes 2211840 | tf_op jit(solution)/shard_map/reduce_scatter | solution.py:286
  398.5 5.7 collective-permute-start.4
  405.5 2.8 copy-start.1
  405.5 3.3 copy-start.8
  405.5 3.3 copy-start.29
  405.5 3.3 copy-start.31
  405.5 3.3 copy-start.33
  408.8 5.5 copy-start.4
  408.8 5.5 copy-start.35
  408.9 5.5 copy-start.55
  408.9 5.5 copy-start.57
  408.9 5.5 copy-start.58
  417.1 5.4 copy-start.16
  417.1 149.3 %all-reduce.12.cloned.1.call-start = ((), (), s32[]{:S(2)}) async-start(), calls=%async_computation.15 | async-start | bytes 6291456 | tf_op jit(solution)/shard_map/psum | solution.py:173
  428.2 112.0 %copy-start.42 = (f32[3,384]{1,0:T(4,128)S(1)}, f32[3,384]{1,0:T(4,128)}, u32[]{:S(2)}) copy-start(f32[3,384]{1,0:T(4,128)} %get-tuple-element.481) | copy-start | bytes 13828
  428.2 112.0 %copy-start.43 = (f32[3,384]{1,0:T(4,128)S(1)}, f32[3,384]{1,0:T(4,128)}, u32[]{:S(2)}) copy-start(f32[3,384]{1,0:T(4,128)} %get-tuple-element.482) | copy-start | bytes 13828
  428.2 112.0 %copy-start.44 = (f32[3,384]{1,0:T(4,128)S(1)}, f32[3,384]{1,0:T(4,128)}, u32[]{:S(2)}) copy-start(f32[3,384]{1,0:T(4,128)} %get-tuple-element.483) | copy-start | bytes 13828
  428.2 138.3 %copy-start.37 = (f32[1,2,2,128]{3,1,2,0:T(2,128)S(1)}, f32[1,2,2,128]{3,1,2,0:T(2,128)}, u32[]{:S(2)}) copy-start(f32[1,2,2,128]{3,1,2,0:T(2,128)} %copy-done.36) | copy-start | bytes 6148
  428.2 138.3 %copy-start.39 = (f32[1,2,2,128]{3,1,2,0:T(2,128)S(1)}, f32[1,2,2,128]{3,1,2,0:T(2,128)}, u32[]{:S(2)}) copy-start(f32[1,2,2,128]{3,1,2,0:T(2,128)} %copy-done.38) | copy-start | bytes 6148
  428.2 140.4 %copy-start.48 = (f32[768]{0:T(1024)S(1)}, f32[768]{0:T(1024)}, u32[]{:S(2)}) copy-start(f32[768]{0:T(1024)} %get-tuple-element.484) | copy-start | bytes 9220
  428.3 140.4 %copy-start.49 = (f32[768]{0:T(1024)S(1)}, f32[768]{0:T(1024)}, u32[]{:S(2)}) copy-start(f32[768]{0:T(1024)} %get-tuple-element.491) | copy-start | bytes 9220
  428.3 226.6 %all-reduce.14.cloned.1.call-start = ((), (), s32[]{:S(2)}) async-start(), calls=%async_computation.16 | async-start | bytes 3538944 | tf_op jit(solution)/shard_map/psum | solution.py:289
  650.6 2.6 copy-start.7
  650.6 2.6 copy-start.11
  654.9 5.9 copy-start.23
  (15 other events, 19.1 us)
Sparse Core Ops, SparseCore 0:
  53.3 64.4 all-gather.3
  140.8 18.5 all-reduce.7
  225.7 20.3 all-reduce.9
  282.6 111.9 reduce-scatter.5
  397.9 25.8 reduce-scatter.9
  426.7 37.3 reduce-scatter.13
  467.2 37.3 reduce-scatter.11
  507.6 32.4 reduce-scatter.7
  543.1 23.3 all-reduce.11
  569.0 78.6 all-reduce.13
Sparse Core Ops, SparseCore 1:
  143.0 35.4 all-gather.5
  180.2 37.2 all-gather.7
